TPU v7x, 32 devices: a whole 2x2x4 slice. The times are simulated.
32 devices in a mesh: cell: 16 (over z, y, x), gene: 2 (over core).
Axes of the slice: x: 2, y: 2, z: 4, core: 2. Of those that a mesh axis runs over, the one named last changes fastest.
Arguments:
- tiles: bfloat16 [2, 1024, 128, 128], P('gene', 'cell'), may hold values from -8 to 8
- tile_row: int32 [2, 1024], P('gene', 'cell'), may hold values from 0 to 7, as said below
- tile_col: int32 [2, 1024], P('gene', 'cell'), may hold values from 0 to 15
- tile_count: int32 [2, 16], P('gene', 'cell'), may hold values from 1 to 64, as said below
- start_basis: bfloat16 [64, 4096], P(None, 'gene'), may hold values from -0.09375 to 0.09375
Outputs:
- basis: bfloat16 [64, 16384], P(None, 'cell')
- loadings: float32 [64, 4096], P(None, ('gene', 'cell'))
Inputs may be any that keep to these rules, and one draw needn't show every extreme that they name: `tile_row`: tile row of each slot, within 0 to 7; the slots of one device name distinct (row, column) pairs. `tile_count`: slots in use; for each index of gene some device uses all 64.
All inputs are finite; a program needn't handle non-finite values.
Results may differ from a plain program's by a relative error of at most 0.018.
Values may be sent and summed in bfloat16 or wider, within the bound.
No kernel may reach another device: no remote copies, remote signals or barrier semaphores. Data moves between devices by JAX's collectives and lax.ppermute only.
A program may use at most 64 MiB of HBM per device.

v0:
```python
import jax
import jax.numpy as jnp
from jax import lax
from jax.sharding import PartitionSpec as P

ROW_BLOCKS = 8


def solve_lower(lower, right):
    return lax.linalg.triangular_solve(lower, right, left_side=True, lower=True)


def gram_of(scores):
    return jnp.dot(
        scores, scores.T, precision=lax.Precision.HIGHEST, preferred_element_type=jnp.float32
    )


def orthonormal(scores, first_total):
    first = first_total(gram_of(scores))
    lower_one = jnp.linalg.cholesky(first)
    return solve_lower(lower_one, scores)


def local(tiles, tile_row, tile_col, tile_count, start_basis):
    blocks_local = tiles[0]
    slot_count = blocks_local.shape[0]
    tile_size = blocks_local.shape[-1]
    width = start_basis.shape[0]
    gene_dev = start_basis.shape[1]
    gene_blocks = gene_dev // tile_size
    row_blocks = ROW_BLOCKS
    cell_dev = row_blocks * tile_size
    row_index = tile_row[0]
    col_index = tile_col[0]
    live = jnp.arange(slot_count) < tile_count[0, 0]
    row_target = jnp.where(live, row_index, row_blocks)
    col_target = jnp.where(live, col_index, gene_blocks)

    def first_total(gram):
        return lax.psum(gram, ("cell", "gene"))

    def merge_halves(partial_scores):
        return lax.psum_scatter(partial_scores, "gene", scatter_dimension=1, tiled=True)

    def scores_of(basis):
        picked = jnp.take(basis.reshape(width, gene_blocks, tile_size), col_index, axis=1)
        products = jnp.einsum(
            "ksg,srg->skr", picked, blocks_local, preferred_element_type=jnp.float32
        )
        summed = jax.ops.segment_sum(products, row_target, num_segments=row_blocks + 1)[:row_blocks]
        return merge_halves(jnp.transpose(summed, (1, 0, 2)).reshape(width, cell_dev))

    def loadings_of(ortho_half):
        picked = jnp.take(ortho_half.reshape(width, row_blocks, tile_size), row_index, axis=1)
        products = jnp.einsum(
            "ksr,srg->skg", picked, blocks_local, preferred_element_type=jnp.float32
        )
        summed = jax.ops.segment_sum(products, col_target, num_segments=gene_blocks + 1)[
            :gene_blocks
        ]
        return jnp.transpose(summed, (1, 0, 2)).reshape(width, gene_dev)

    ortho = orthonormal(scores_of(start_basis), first_total)
    ortho_half = ortho.astype(jnp.bfloat16)
    ortho_rows = lax.all_gather(ortho_half, "gene", axis=1, tiled=True)
    partial_value = loadings_of(ortho_rows)
    next_basis = lax.psum(partial_value, "cell").astype(jnp.bfloat16)
    ortho_two = orthonormal(scores_of(next_basis), first_total)
    scale = jnp.sqrt(jnp.float32(lax.axis_size("cell") * cell_dev))
    ortho_two_half = ortho_two.astype(jnp.bfloat16)
    basis_piece = (ortho_two * scale).astype(jnp.bfloat16)
    final_rows, basis = (
        lax.all_gather(ortho_two_half, "gene", axis=1, tiled=True),
        lax.all_gather(basis_piece, "gene", axis=1, tiled=True),
    )
    loadings = lax.psum_scatter(loadings_of(final_rows), "cell", scatter_dimension=1, tiled=True)
    return (basis, loadings)


def solution(mesh):
    return jax.shard_map(
        local,
        mesh=mesh,
        in_specs=(
            P("gene", "cell", None, None),
            P("gene", "cell"),
            P("gene", "cell"),
            P("gene", "cell"),
            P(None, "gene"),
        ),
        out_specs=(P(None, "cell"), P(None, ("gene", "cell"))),
        check_vma=False,
    )
```

profile of v0, /device:TPU:0, one launch (start us, length us, event | category | flops | bytes accessed | tf_op | source)
XLA Modules:
  0.0 349.9 jit_solution(15291023441210544630)
XLA Ops:
  11.2 2.9 fusion.6
  14.1 7.1 %scatter_fusion = f32[9,64,128]{2,1,0:T(8,128)S(1)} fusion(f32[9,64,128]{2,1,0:T(8,128)S(1)} %broadcast.69.clone, s32[64]{0:T(128)S(1)} %get-tuple-element.8, f32[64,64,128]{2,1,0:T(8,128)} %fusion.6), kind=kCustom, calls=%fused_computation.4 | custom fusion | flops 524288 | bytes 6291712 | tf_op jit(solution)/shard_map/scatter-add | solution.py:51
  22.0 10.5 %reduce-scatter.4.cloned.1.call-done = f32[64,512]{1,0:T(8,128)} async-done(((f32[64,1024]{1,0:T(8,128)}), f32[64,512]{1,0:T(8,128)}) %reduce-scatter.4.cloned.1.call-update) | async-done | bytes 131088 | tf_op jit(solution)/shard_map/reduce_scatter | solution.py:44
  32.5 1.2 fusion.40
  33.8 40.5 %psum.21 = f32[64,64]{0,1:T(8,128)S(1)} all-reduce(f32[64,64]{0,1:T(8,128)S(1)} %fusion.40), channel_id=1, replica_groups=mesh['cell'=16,'gene'=2] {'cell','gene'}, use_global_device_ids=true, to_apply=%region_2.4 | all-reduce | flops 4096 | bytes 32768 | tf_op jit(solution)/shard_map/psum | solution.py:41
  74.4 5.8 %cholesky.44 = f32[64,64]{1,0:T(8,128)S(1)} custom-call(f32[64,64]{1,0:T(8,128)S(1)} %fusion.30), custom_call_target="Cholesky" | custom-call | tf_op jit(solution)/shard_map/jit(cholesky)/cholesky | solution.py:21
  81.6 4.9 %custom-call.6 = f32[1,64,64]{1,2,0:T(8,128)S(1)} custom-call(f32[1,64,64]{2,1,0:T(8,128)S(1)} %fusion.24), custom_call_target="InvertDiagBlocksLowerTriangular" | custom-call | tf_op jit(solution)/shard_map/triangular_solve/custom-call.0 | solution.py:10
  86.5 1.2 convolution_convert_fusion
  87.7 1.9 all_gather.9
  90.4 2.1 fusion.4
  92.6 7.1 %scatter_fusion.1 = f32[17,64,128]{2,1,0:T(8,128)S(1)} fusion(f32[17,64,128]{2,1,0:T(8,128)S(1)} %broadcast.70.clone, s32[64]{0:T(128)S(1)} %get-tuple-element.9, f32[64,64,128]{2,1,0:T(8,128)} %fusion.4), kind=kCustom, calls=%fused_computation.5 | custom fusion | flops 524288 | bytes 6291712 | tf_op jit(solution)/shard_map/scatter-add | solution.py:59
  99.7 81.7 %all-reduce.1 = bf16[64,2048]{1,0:T(8,128)(2,1)S(1)} all-reduce(f32[64,2048]{1,0:T(8,128)S(1)} %copy_bitcast_fusion.1), channel_id=1, replica_groups=mesh['cell'=16,'gene'=2] {'cell'}, use_global_device_ids=true, to_apply=%region_6.11 | all-reduce | flops 131072 | bytes 786432 | tf_op jit(solution)/shard_map/psum | solution.py:68
  182.2 2.9 fusion.2
  185.1 7.1 %scatter_fusion.2 = f32[9,64,128]{2,1,0:T(8,128)S(1)} fusion(f32[9,64,128]{2,1,0:T(8,128)S(1)} %broadcast.69, s32[64]{0:T(128)S(1)} %get-tuple-element.8, f32[64,64,128]{2,1,0:T(8,128)} %fusion.2), kind=kCustom, calls=%fused_computation.6 | custom fusion | flops 524288 | bytes 6291712 | tf_op jit(solution)/shard_map/scatter-add | solution.py:51
  192.9 4.2 %reduce-scatter.6.cloned.1.call-done = f32[64,512]{1,0:T(8,128)} async-done(((f32[64,1024]{1,0:T(8,128)}), f32[64,512]{1,0:T(8,128)}) %reduce-scatter.6.cloned.1.call-update) | async-done | bytes 131088 | tf_op jit(solution)/shard_map/reduce_scatter | solution.py:44
  198.4 40.8 %psum.23 = f32[64,64]{0,1:T(8,128)S(1)} all-reduce(f32[64,64]{0,1:T(8,128)S(1)} %fusion.41), channel_id=1, replica_groups=mesh['cell'=16,'gene'=2] {'cell','gene'}, use_global_device_ids=true, to_apply=%region_9.14 | all-reduce | flops 4096 | bytes 32768 | tf_op jit(solution)/shard_map/psum | solution.py:41
  239.2 5.8 %cholesky.55 = f32[64,64]{1,0:T(8,128)S(1)} custom-call(f32[64,64]{1,0:T(8,128)S(1)} %fusion.28), custom_call_target="Cholesky" | custom-call | tf_op jit(solution)/shard_map/jit(cholesky)/cholesky | solution.py:21
  246.4 4.9 %custom-call.7 = f32[1,64,64]{1,2,0:T(8,128)S(1)} custom-call(f32[1,64,64]{2,1,0:T(8,128)S(1)} %fusion.25), custom_call_target="InvertDiagBlocksLowerTriangular" | custom-call | tf_op jit(solution)/shard_map/triangular_solve/custom-call.0 | solution.py:10
  251.3 1.2 fusion.39
  252.6 1.9 all_gather.11
  255.2 2.1 fusion
  257.4 7.1 %scatter_fusion.3 = f32[17,64,128]{2,1,0:T(8,128)S(1)} fusion(f32[17,64,128]{2,1,0:T(8,128)S(1)} %broadcast.70, s32[64]{0:T(128)S(1)} %get-tuple-element.9, f32[64,64,128]{2,1,0:T(8,128)} %fusion), kind=kCustom, calls=%fused_computation.7 | custom fusion | flops 524288 | bytes 6291712 | tf_op jit(solution)/shard_map/scatter-add | solution.py:59
  265.3 1.9 all_gather.10
  267.2 75.5 %reduce-scatter.8.cloned.1.call-done = f32[64,128]{1,0:T(8,128)} async-done(((f32[64,2048]{1,0:T(8,128)}), f32[64,128]{1,0:T(8,128)}) %reduce-scatter.8.cloned.1.call-update) | async-done | bytes 32784 | tf_op jit(solution)/shard_map/reduce_scatter | solution.py:77
  (47 shorter events, 12.9 us)
Async XLA Ops:
  7.2 4.0 %copy-start = (bf16[1,64,128,128]{3,2,1,0:T(8,128)(2,1)S(1)}, bf16[1,64,128,128]{3,2,1,0:T(8,128)(2,1)}, u32[]{:S(2)}) copy-start(bf16[1,64,128,128]{3,2,1,0:T(8,128)(2,1)} %param.12) | copy-start | bytes 6291460
  7.2 4.0 %copy-start.1 = (s32[1,64]{1,0:T(1,128)S(1)}, s32[1,64]{1,0:T(1,128)}, u32[]{:S(2)}) copy-start(s32[1,64]{1,0:T(1,128)} %param.14) | copy-start | bytes 772
  7.2 4.0 %copy-start.2 = (s32[1,64]{1,0:T(1,128)S(1)}, s32[1,64]{1,0:T(1,128)}, u32[]{:S(2)}) copy-start(s32[1,64]{1,0:T(1,128)} %param.13) | copy-start | bytes 772
  7.2 25.3 %reduce-scatter.4.cloned.1.call-start = ((), (), s32[]{:S(2)}) async-start(), calls=%async_computation.3 | async-start | bytes 393216 | tf_op jit(solution)/shard_map/reduce_scatter | solution.py:44
  21.9 175.2 %reduce-scatter.6.cloned.1.call-start = ((), (), s32[]{:S(2)}) async-start(), calls=%async_computation.4 | async-start | bytes 393216 | tf_op jit(solution)/shard_map/reduce_scatter | solution.py:44
  192.9 149.8 %reduce-scatter.8.cloned.1.call-start = ((), (), s32[]{:S(2)}) async-start(), calls=%async_computation.5 | async-start | bytes 557056 | tf_op jit(solution)/shard_map/reduce_scatter | solution.py:77
Sparse Core Ops, SparseCore 0:
  22.0 10.4 reduce-scatter.3
  193.0 4.0 reduce-scatter.5
  265.4 77.2 reduce-scatter.7
where the time goes:
time: 351 us; the launch traced here: 350 us
  blocking collectives  169 us (48%)
  waiting for transfers between devices  90.3 us (26%)
  other arithmetic  53.9 us (15%)
  matrix products  14.9 us (4%)
  between operations  14.7 us (4%)
  local copies, waits for them, and re-layouts  7.35 us (2%)
    psum x1, blocking collectives, local(): next_basis = lax.psum(partial_value, 'cell').astype(jnp.bfloat16)  81.7 us
    psum x2, blocking collectives, first_total(): return lax.psum(gram, ('cell', 'gene'))  81.3 us
    reduce_scatter x1, waiting for transfers between devices, local(): lax.psum_scatter(loadings_of(final_rows), 'cell', scatter_dimension=1, ti...  75.5 us
    reduce_scatter x2, waiting for transfers between devices, merge_halves(): lax.psum_scatter(partial_scores, 'gene', scatter_dimension=1, tiled=True)  14.7 us
    scatter-add x2, other arithmetic, scores_of(): jax.ops.segment_sum(products, row_target, num_segments=row_blocks + 1)  14.1 us
    scatter-add x2, other arithmetic, loadings_of(): jax.ops.segment_sum(products, col_target, num_segments=gene_blocks + 1)  14.1 us
    another operation x6, other arithmetic, orthonormal(): lower_one = jnp.linalg.cholesky(first)  13 us
    another operation x4, other arithmetic, solve_lower(): return lax.linalg.triangular_solve(lower, right, left_side=True, lower=True)  11.1 us
  transfers between devices with their start and end apart: 3, of which 3 were waited for; matrix products, arithmetic and copies ran while one was open for 0% of the time, Pallas kernels for 0%

commit v1 on v0

--- a/solution.py
+++ b/solution.py
@@ -38,7 +38,7 @@
     col_target = jnp.where(live, col_index, gene_blocks)
 
     def first_total(gram):
-        return lax.psum(gram, ("cell", "gene"))
+        return lax.psum(lax.psum(gram, "gene"), "cell")
 
     def merge_halves(partial_scores):
         return lax.psum_scatter(partial_scores, "gene", scatter_dimension=1, tiled=True)

time: 351 us -> 425 us (1.21)
  blocking collectives: 169 us -> 244 us
    psum x2 -> x4, blocking collectives: 81.3 us -> 161 us  [first_total(): return lax.psum(lax.psum(gram, 'gene'), 'cell')]
    psum x1, blocking collectives: 81.7 us -> 77.3 us  [local(): next_basis = lax.psum(partial_value, 'cell').astype(jnp.bfloat16)]
where the time goes in v1:
time: 425 us; the launch traced here: 423 us
  blocking collectives  244 us (57%)
  waiting for transfers between devices  88.4 us (21%)
  other arithmetic  53.9 us (13%)
  matrix products  14.9 us (4%)
  between operations  14.7 us (3%)
  local copies, waits for them, and re-layouts  7.35 us (2%)
    psum x4, blocking collectives, first_total(): return lax.psum(lax.psum(gram, 'gene'), 'cell')  161 us
    psum x1, blocking collectives, local(): next_basis = lax.psum(partial_value, 'cell').astype(jnp.bfloat16)  77.3 us
    reduce_scatter x1, waiting for transfers between devices, local(): lax.psum_scatter(loadings_of(final_rows), 'cell', scatter_dimension=1, ti...  71.8 us
    reduce_scatter x2, waiting for transfers between devices, merge_halves(): lax.psum_scatter(partial_scores, 'gene', scatter_dimension=1, tiled=True)  16.6 us
    scatter-add x2, other arithmetic, scores_of(): jax.ops.segment_sum(products, row_target, num_segments=row_blocks + 1)  14.1 us
    scatter-add x2, other arithmetic, loadings_of(): jax.ops.segment_sum(products, col_target, num_segments=gene_blocks + 1)  14.1 us
    another operation x6, other arithmetic, orthonormal(): lower_one = jnp.linalg.cholesky(first)  13 us
    another operation x4, other arithmetic, solve_lower(): return lax.linalg.triangular_solve(lower, right, left_side=True, lower=True)  11.1 us
  transfers between devices with their start and end apart: 3, of which 3 were waited for; matrix products, arithmetic and copies ran while one was open for 0% of the time, Pallas kernels for 0%

profile of v1, /device:TPU:0, one launch (start us, length us, event | category | flops | bytes accessed | tf_op | source)
XLA Modules:
  0.0 423.5 jit_solution(1674512681813735329)
XLA Ops:
  11.2 2.9 fusion.6
  14.1 7.1 %scatter_fusion = f32[9,64,128]{2,1,0:T(8,128)S(1)} fusion(f32[9,64,128]{2,1,0:T(8,128)S(1)} %broadcast.69.clone, s32[64]{0:T(128)S(1)} %get-tuple-element.8, f32[64,64,128]{2,1,0:T(8,128)} %fusion.6), kind=kCustom, calls=%fused_computation.4 | custom fusion | flops 524288 | bytes 6291712 | tf_op jit(solution)/shard_map/scatter-add | solution.py:51
  22.0 10.5 %reduce-scatter.4.cloned.1.call-done = f32[64,512]{1,0:T(8,128)} async-done(((f32[64,1024]{1,0:T(8,128)}), f32[64,512]{1,0:T(8,128)}) %reduce-scatter.4.cloned.1.call-update) | async-done | bytes 131088 | tf_op jit(solution)/shard_map/reduce_scatter | solution.py:44
  33.8 3.4 psum.35
  37.2 77.1 %psum.36 = f32[64,64]{0,1:T(8,128)S(1)} all-reduce(f32[64,64]{0,1:T(8,128)S(1)} %psum.35), channel_id=1, replica_groups=mesh['cell'=16,'gene'=2] {'cell'}, use_global_device_ids=true, to_apply=%region_3.5 | all-reduce | flops 4096 | bytes 32768 | tf_op jit(solution)/shard_map/psum | solution.py:41
  114.4 5.8 %cholesky.44 = f32[64,64]{1,0:T(8,128)S(1)} custom-call(f32[64,64]{1,0:T(8,128)S(1)} %fusion.30), custom_call_target="Cholesky" | custom-call | tf_op jit(solution)/shard_map/jit(cholesky)/cholesky | solution.py:21
  121.6 4.9 %custom-call.6 = f32[1,64,64]{1,2,0:T(8,128)S(1)} custom-call(f32[1,64,64]{2,1,0:T(8,128)S(1)} %fusion.24), custom_call_target="InvertDiagBlocksLowerTriangular" | custom-call | tf_op jit(solution)/shard_map/triangular_solve/custom-call.0 | solution.py:10
  127.7 1.9 all_gather.9
  130.4 2.1 fusion.4
  132.6 7.1 %scatter_fusion.1 = f32[17,64,128]{2,1,0:T(8,128)S(1)} fusion(f32[17,64,128]{2,1,0:T(8,128)S(1)} %broadcast.70.clone, s32[64]{0:T(128)S(1)} %get-tuple-element.9, f32[64,64,128]{2,1,0:T(8,128)} %fusion.4), kind=kCustom, calls=%fused_computation.5 | custom fusion | flops 524288 | bytes 6291712 | tf_op jit(solution)/shard_map/scatter-add | solution.py:59
  139.7 77.3 %all-reduce.1 = bf16[64,2048]{1,0:T(8,128)(2,1)S(1)} all-reduce(f32[64,2048]{1,0:T(8,128)S(1)} %copy_bitcast_fusion.1), channel_id=1, replica_groups=mesh['cell'=16,'gene'=2] {'cell'}, use_global_device_ids=true, to_apply=%region_7.12 | all-reduce | flops 131072 | bytes 786432 | tf_op jit(solution)/shard_map/psum | solution.py:68
  217.8 2.9 fusion.2
  220.7 7.1 %scatter_fusion.2 = f32[9,64,128]{2,1,0:T(8,128)S(1)} fusion(f32[9,64,128]{2,1,0:T(8,128)S(1)} %broadcast.69, s32[64]{0:T(128)S(1)} %get-tuple-element.8, f32[64,64,128]{2,1,0:T(8,128)} %fusion.2), kind=kCustom, calls=%fused_computation.6 | custom fusion | flops 524288 | bytes 6291712 | tf_op jit(solution)/shard_map/scatter-add | solution.py:51
  228.5 6.1 %reduce-scatter.6.cloned.1.call-done = f32[64,512]{1,0:T(8,128)} async-done(((f32[64,1024]{1,0:T(8,128)}), f32[64,512]{1,0:T(8,128)}) %reduce-scatter.6.cloned.1.call-update) | async-done | bytes 131088 | tf_op jit(solution)/shard_map/reduce_scatter | solution.py:44
  235.9 3.4 psum.38
  239.3 77.1 %psum.39 = f32[64,64]{0,1:T(8,128)S(1)} all-reduce(f32[64,64]{0,1:T(8,128)S(1)} %psum.38), channel_id=1, replica_groups=mesh['cell'=16,'gene'=2] {'cell'}, use_global_device_ids=true, to_apply=%region_11.16 | all-reduce | flops 4096 | bytes 32768 | tf_op jit(solution)/shard_map/psum | solution.py:41
  316.6 5.8 %cholesky.55 = f32[64,64]{1,0:T(8,128)S(1)} custom-call(f32[64,64]{1,0:T(8,128)S(1)} %fusion.28), custom_call_target="Cholesky" | custom-call | tf_op jit(solution)/shard_map/jit(cholesky)/cholesky | solution.py:21
  323.7 4.9 %custom-call.7 = f32[1,64,64]{1,2,0:T(8,128)S(1)} custom-call(f32[1,64,64]{2,1,0:T(8,128)S(1)} %fusion.25), custom_call_target="InvertDiagBlocksLowerTriangular" | custom-call | tf_op jit(solution)/shard_map/triangular_solve/custom-call.0 | solution.py:10
  328.6 1.2 fusion.39
  329.9 1.9 all_gather.11
  332.6 2.1 fusion
  334.7 7.1 %scatter_fusion.3 = f32[17,64,128]{2,1,0:T(8,128)S(1)} fusion(f32[17,64,128]{2,1,0:T(8,128)S(1)} %broadcast.70, s32[64]{0:T(128)S(1)} %get-tuple-element.9, f32[64,64,128]{2,1,0:T(8,128)} %fusion), kind=kCustom, calls=%fused_computation.7 | custom fusion | flops 524288 | bytes 6291712 | tf_op jit(solution)/shard_map/scatter-add | solution.py:59
  342.6 1.9 all_gather.10
  344.5 71.8 %reduce-scatter.8.cloned.1.call-done = f32[64,128]{1,0:T(8,128)} async-done(((f32[64,2048]{1,0:T(8,128)}), f32[64,128]{1,0:T(8,128)}) %reduce-scatter.8.cloned.1.call-update) | async-done | bytes 32784 | tf_op jit(solution)/shard_map/reduce_scatter | solution.py:77
  (49 shorter events, 15.4 us)
Async XLA Ops:
  7.2 4.0 copy-start
  7.2 4.0 copy-start.1
  7.2 4.0 copy-start.2
  7.2 25.3 %reduce-scatter.4.cloned.1.call-start = ((), (), s32[]{:S(2)}) async-start(), calls=%async_computation.3 | async-start | bytes 393216 | tf_op jit(solution)/shard_map/reduce_scatter | solution.py:44
  21.9 212.8 %reduce-scatter.6.cloned.1.call-start = ((), (), s32[]{:S(2)}) async-start(), calls=%async_computation.4 | async-start | bytes 393216 | tf_op jit(solution)/shard_map/reduce_scatter | solution.py:44
  228.5 187.8 %reduce-scatter.8.cloned.1.call-start = ((), (), s32[]{:S(2)}) async-start(), calls=%async_computation.5 | async-start | bytes 557056 | tf_op jit(solution)/shard_map/reduce_scatter | solution.py:77
Sparse Core Ops, SparseCore 0:
  22.0 10.4 reduce-scatter.3
  228.6 5.9 reduce-scatter.5
  342.7 73.4 reduce-scatter.7
